TPU v7x, 32 devices: a whole 2x2x4 slice. The times are simulated.
32 devices in a mesh: chain: 16 (over z, y, x), grp: 2 (over core).
Axes of the slice: x: 2, y: 2, z: 4, core: 2. Of those that a mesh axis runs over, the one named last changes fastest.
Arguments:
- codes: bfloat16 [2, 16384, 6144], P(None, ('chain', 'grp')), may hold values from -6 to 6
- exponents: int32 [2, 512, 6144], P(None, ('chain', 'grp')), may hold values from -2 to 2
- column_map: int32 [32], replicated, may hold values from 0 to 31, each once
- row_order: int32 [32], replicated, may hold values from 0 to 31, each once
Outputs:
- rollout: bfloat16 [2, 6144, 16384], P(None, ('chain', 'grp'))
- block_sums: float32 [2, 6144, 512], P(None, ('chain', 'grp'))
All inputs are finite; a program needn't handle non-finite values.
Results may differ from a plain program's by a relative error of at most 0.001.
Values may be sent and summed in bfloat16 or wider, within the bound.
A program may use at most 128 MiB of HBM per device.

v0:
```python
import jax
import jax.numpy as jnp
from jax import lax
from jax.sharding import PartitionSpec as P


def arrange(array, column_map, devices, col_width):
    layer_count, row_count, _ = array.shape
    order = (
        jnp.arange(col_width, dtype=jnp.int32)[:, None] + column_map[None, :] * col_width
    ).reshape(-1)
    picked = jnp.take(array, order, axis=2)
    return jnp.swapaxes(picked, 1, 2).reshape(layer_count, col_width, devices, row_count)


def shards(codes, exponents, column_map, row_order):
    chain_size = lax.axis_size("chain")
    grp_size = lax.axis_size("grp")
    devices = chain_size * grp_size
    layer_count, row_count, width_all = codes.shape
    col_width = width_all // devices
    scaling = jnp.exp2(exponents.astype(jnp.float32))
    values = (codes.astype(jnp.float32) * jnp.repeat(scaling, 32, axis=1)).astype(jnp.bfloat16)
    outgoing = arrange(values, column_map, devices, col_width)
    width = outgoing.shape[3]
    shaped = outgoing.reshape(layer_count, col_width, chain_size, grp_size, width)
    arrived = lax.all_to_all(
        lax.all_to_all(shaped, "chain", split_axis=2, concat_axis=2, tiled=True),
        "grp",
        split_axis=3,
        concat_axis=3,
        tiled=True,
    )
    arrived = arrived.reshape(layer_count, col_width, devices, width)
    values = arrived
    values = jnp.take(values, row_order, axis=2)
    rollout = values.reshape(layer_count, col_width, devices * row_count)
    block_sums = (
        rollout.astype(jnp.float32)
        .reshape(layer_count, col_width, devices * row_count // 32, 32)
        .sum(axis=-1)
    )
    return (rollout, block_sums)


def solution(mesh):
    return jax.shard_map(
        shards,
        mesh=mesh,
        in_specs=(P(None, ("chain", "grp"), None), P(None, ("chain", "grp"), None), P(), P()),
        out_specs=(P(None, ("chain", "grp"), None), P(None, ("chain", "grp"), None)),
        check_vma=False,
    )
```

profile of v0, /device:TPU:15, one launch (start us, length us, event | category | flops | bytes accessed | tf_op | source)
XLA Modules:
  0.0 536.4 jit_solution(8782882133313919337)
XLA Ops:
  0.6 0.7 broadcast_multiply_fusion
  1.3 0.1 add.66
  1.4 0.1 add.63
  1.6 1.2 multiply_exponential_fusion
  2.8 11.6 %fusion = bf16[2,512,6144]{2,1,0:T(8,128)(2,1)} fusion(bf16[2,512,6144]{2,1,0:T(8,128)(2,1)} %param.4, f32[2,16,6144]{2,1,0:T(8,128)S(1)} %multiply_exponential_fusion), kind=kLoop, calls=%fused_computation.4 | loop fusion | flops 18874368 | bytes 25952256 | tf_op jit(solution)/shard_map/convert_element_type | solution.py:23
  14.5 31.0 %copy.26 = bf16[2,512,6144]{1,0,2:T(2,128)(2,1)} copy(bf16[2,512,6144]{2,1,0:T(8,128)(2,1)} %fusion) | data formatting | bytes 25165824 | tf_op jit(solution)/shard_map/convert_element_type | solution.py:23
  45.4 67.6 %gather_fusion = bf16[6144,2,512]{2,1,0:T(2,128)(2,1)} fusion(bf16[2,512,6144]{1,0,2:T(2,128)(2,1)} %copy.26, s32[6144]{0:T(1024)S(1)} %broadcast_clamp_fusion), kind=kCustom, calls=%fused_computation | custom fusion | bytes 25190400 | tf_op jit(solution)/shard_map/jit(_take)/gather | solution.py:12
  113.0 23.6 %broadcast_select_fusion = bf16[6144,2,512]{2,1,0:T(2,128)(2,1)S(1)} fusion(bf16[6144,2,512]{2,1,0:T(2,128)(2,1)} %gather_fusion, pred[6144]{0:T(1024)(128)(4,1)S(1)} %compare_and_fusion), kind=kLoop, calls=%fused_computation.5 | loop fusion | flops 6291456 | bytes 25171968 | tf_op jit(solution)/shard_map/jit(_take)/select_n | solution.py:12
  136.6 10.1 %copy.27 = bf16[2,192,16,2,512]{4,0,3,1,2:T(2,128)(2,1)} copy(bf16[2,192,16,2,512]{4,0,3,2,1:T(2,128)(2,1)S(1)} %bitcast.21) | data formatting | bytes 25165824 | tf_op jit(solution)/shard_map/reshape;reshape | solution.py:26
  146.8 0.0 copy-start
  146.8 6.7 %all-to-all-start = ((bf16[2,192,16,2,512]{4,0,3,1,2:T(2,128)(2,1)}), bf16[2,192,16,2,512]{4,0,3,1,2:T(2,128)(2,1)}, u32[]{:S(2)}, u32[]{:S(2)}) async-start(bf16[2,192,16,2,512]{4,0,3,1,2:T(2,128)(2,1)} %copy.27), calls=%async_computation | async-start | bytes 25165824 | tf_op jit(solution)/shard_map/all_to_all | solution.py:28
  153.5 0.0 copy-done
  153.5 0.1 broadcast_in_dim.47
  153.6 0.1 broadcast_in_dim.48
  153.7 0.1 broadcast_bitcast_fusion
  153.8 281.7 %all-to-all-done = bf16[2,192,16,2,512]{4,0,3,1,2:T(2,128)(2,1)} async-done(((bf16[2,192,16,2,512]{4,0,3,1,2:T(2,128)(2,1)}), bf16[2,192,16,2,512]{4,0,3,1,2:T(2,128)(2,1)}, u32[]{:S(2)}, u32[]{:S(2)}) %all-to-all-start) | async-done | bytes 12582944 | tf_op jit(solution)/shard_map/all_to_all | solution.py:28
  435.6 13.3 %copy.28 = bf16[2,192,16,2,512]{4,0,2,1,3:T(2,128)(2,1)S(1)} copy(bf16[2,192,16,2,512]{4,0,3,1,2:T(2,128)(2,1)} %all-to-all-done) | data formatting | bytes 25165824 | tf_op jit(solution)/shard_map/all_to_all | solution.py:28
  448.8 14.9 %all_to_all.10 = bf16[2,192,16,2,512]{4,0,2,1,3:T(2,128)(2,1)S(1)} all-to-all(bf16[2,192,16,2,512]{4,0,2,1,3:T(2,128)(2,1)S(1)} %copy.28), channel_id=1, replica_groups=mesh['chain'=16,'grp'=2] {'grp'}, dimensions={3} | all-to-all | bytes 25165824 | tf_op jit(solution)/shard_map/all_to_all | solution.py:27
  463.7 10.0 %copy.34 = bf16[2,192,16,2,512]{4,1,0,3,2:T(8,128)(2,1)} copy(bf16[2,192,16,2,512]{4,0,2,1,3:T(2,128)(2,1)S(1)} %all_to_all.10) | data formatting | bytes 25165824 | tf_op jit(solution)/shard_map/reshape | solution.py:34
  473.7 11.4 %gather_fusion.1 = bf16[32,2,192,512]{3,2,1,0:T(8,128)(2,1)} fusion(bf16[2,192,32,512]{3,1,0,2:T(8,128)(2,1)} %bitcast.22, s32[1024]{0:T(1024)S(1)} %pad_clamp_fusion), kind=kCustom, calls=%fused_computation.1 | custom fusion | bytes 25165952 | tf_op jit(solution)/shard_map/jit(_take)/gather | solution.py:36
  485.1 10.6 %copy.35 = bf16[32,2,24,8,512]{4,3,0,2,1:T(8,128)(2,1)} copy(bf16[32,2,24,8,512]{4,3,2,1,0:T(8,128)(2,1)} %bitcast.17) | data formatting | bytes 25165824 | tf_op jit(solution)/shard_map/jit(_take)/gather | solution.py:36
  495.7 19.5 %copy.32 = bf16[2,192,32,512]{1,3,2,0:T(8,128)(2,1)} copy(bf16[2,192,32,512]{3,1,0,2:T(8,128)(2,1)} %bitcast.18) | data formatting | bytes 25165824 | tf_op jit(solution)/shard_map/jit(_take)/gather | solution.py:36
  515.3 9.2 %convert_reduce_fusion = f32[2,192,512]{1,2,0:T(8,128)S(1)} fusion(bf16[2,192,512,32]{1,3,2,0:T(8,128)(2,1)} %bitcast.19, pred[512]{0:T(512)(128)(4,1)S(1)} %broadcast_in_dim.48), kind=kLoop, calls=%fused_computation.2 | loop fusion | flops 18677760 | bytes 13369856 | tf_op jit(solution)/shard_map/reduce_sum | solution.py:41
  524.5 1.2 copy.33
  525.7 10.7 %broadcast_select_fusion.1 = bf16[2,192,16384]{2,1,0:T(8,128)(2,1)} fusion(bf16[2,192,16384]{2,1,0:T(8,128)(2,1)} %bitcast.20, pred[16384]{0:T(1024)(128)(4,1)S(1)} %bitcast.24), kind=kLoop, calls=%fused_computation.6 | loop fusion | flops 6291456 | bytes 25182208 | tf_op jit(solution)/shard_map/jit(_take)/select_n | solution.py:36
  (8 shorter events, 0.1 us)
Async XLA Ops:
  146.8 6.7 %copy-start = (s32[32]{0:T(128)S(1)}, s32[32]{0:T(128)}, u32[]{:S(2)}) copy-start(s32[32]{0:T(128)} %param.7) | copy-start | bytes 388
  146.8 288.8 %all-to-all-start = ((bf16[2,192,16,2,512]{4,0,3,1,2:T(2,128)(2,1)}), bf16[2,192,16,2,512]{4,0,3,1,2:T(2,128)(2,1)}, u32[]{:S(2)}, u32[]{:S(2)}) async-start(bf16[2,192,16,2,512]{4,0,3,1,2:T(2,128)(2,1)} %copy.27), calls=%async_computation | async-start | bytes 25165824 | tf_op jit(solution)/shard_map/all_to_all | solution.py:28
where the time goes:
time: 542 us; the launch traced here: 536 us
  waiting for transfers between devices  282 us (52%)
  local copies, waits for them, and re-layouts  175 us (32%)
  other arithmetic  57.2 us (11%)
  blocking collectives  14.9 us (3%)
  starting transfers between devices  6.71 us (1%)
    all_to_all x1, waiting for transfers between devices, shards(): lax.all_to_all(shaped, 'chain', split_axis=2, concat_axis=2, tiled=True)  282 us
    gather x1, local copies, waits for them, and re-layouts, arrange(): picked = jnp.take(array, order, axis=2)  67.6 us
    gather x3, local copies, waits for them, and re-layouts, shards(): values = jnp.take(values, row_order, axis=2)  41.5 us
    convert_element_type x1, local copies, waits for them, and re-layouts, shards(): (codes.astype(jnp.float32) * jnp.repeat(scaling, 32, axis=1)).astype(jnp....  31 us
    select_n x2, other arithmetic, arrange(): picked = jnp.take(array, order, axis=2)  23.6 us
    all_to_all x1, blocking collectives, shards(): lax.all_to_all(lax.all_to_all(shaped, 'chain', split_axis=2, concat_axis=...  14.9 us
    all_to_all x1, local copies, waits for them, and re-layouts, shards(): lax.all_to_all(shaped, 'chain', split_axis=2, concat_axis=2, tiled=True)  13.3 us
    convert_element_type x1, other arithmetic, shards(): (codes.astype(jnp.float32) * jnp.repeat(scaling, 32, axis=1)).astype(jnp....  11.6 us
  transfers between devices with their start and end apart: 1, of which 1 were waited for; matrix products, arithmetic and copies ran while one was open for 0% of the time, Pallas kernels for 0%

commit v1 on v0

v1 whole, which is shorter than its diff:
```python
import functools

import jax
import jax.numpy as jnp
from jax import lax
from jax.experimental import pallas as pl
from jax.experimental.pallas import tpu as pltpu
from jax.sharding import PartitionSpec as P

MESH = pl.DeviceIdType.MESH
BLOCK = 32
LANES = 128


def prepare_kernel(where, codes, exponents, out, held):
    layers, rows, pair = codes.shape
    col_width = pair // 2

    @pl.when(pl.program_id(1) == 0)
    def _():
        for layer in range(layers):
            scaling = jnp.exp2(exponents[layer].astype(jnp.float32)).astype(jnp.bfloat16)
            for first in range(0, rows, LANES):
                pieces = []
                for row in range(first, first + LANES, BLOCK):
                    block = row // BLOCK
                    pieces.append(codes[layer, row : row + BLOCK, :] * scaling[block : block + 1, :])
                turned = jnp.concatenate(pieces, axis=0).T
                out[0, layer, :, first : first + LANES] = turned[:col_width]
                held[layer, :, first : first + LANES] = turned[col_width:]

    @pl.when(pl.program_id(1) == 1)
    def _():
        out[0] = held[...]


def prepare(codes, exponents, column_map, devices):
    layers, rows, width = codes.shape
    col_width = width // devices
    places = jnp.arange(devices, dtype=jnp.int32)
    if col_width % 64 or rows % LANES or devices % 2:
        scaling = jnp.exp2(exponents.astype(jnp.float32))
        values = (codes.astype(jnp.float32) * jnp.repeat(scaling, BLOCK, axis=1)).astype(jnp.bfloat16)
        values = values.reshape(layers, rows, devices, col_width)
        return jnp.take(values.transpose(2, 0, 3, 1), column_map, axis=0)
    where = jnp.sum(jnp.where(column_map[None, :] == places[:, None], places[None, :], 0), axis=1)
    return pl.pallas_call(
        prepare_kernel,
        grid_spec=pltpu.PrefetchScalarGridSpec(
            num_scalar_prefetch=1,
            grid=(devices // 2, 2),
            in_specs=[
                pl.BlockSpec((layers, rows, 2 * col_width), lambda c, j, where: (0, 0, c)),
                pl.BlockSpec((layers, rows // BLOCK, 2 * col_width), lambda c, j, where: (0, 0, c)),
            ],
            out_specs=pl.BlockSpec((1, layers, col_width, rows), lambda c, j, where: (where[2 * c + j], 0, 0, 0)),
            scratch_shapes=[pltpu.VMEM((layers, col_width, rows), jnp.bfloat16)],
        ),
        out_shape=jax.ShapeDtypeStruct((devices, layers, col_width, rows), jnp.bfloat16),
    )(where.astype(jnp.int32), codes, exponents)


def exchange_kernel(devices, grp_size, outgoing, arrived, own, send_sems, recv_sems, own_sems):
    me = lax.axis_index("chain") * grp_size + lax.axis_index("grp")

    def copy_to(step):
        peer = lax.rem(me + step, devices)
        return pltpu.make_async_remote_copy(
            src_ref=outgoing.at[peer],
            dst_ref=arrived.at[me],
            send_sem=send_sems.at[step],
            recv_sem=recv_sems.at[step],
            device_id=(peer // grp_size, lax.rem(peer, grp_size)),
            device_id_type=MESH,
        )

    @pl.loop(1, devices)
    def _(step):
        copy_to(step).start()

    take = pltpu.make_async_copy(outgoing.at[me], own, own_sems.at[0])
    take.start()
    take.wait()
    put = pltpu.make_async_copy(own, arrived.at[me], own_sems.at[1])
    put.start()
    put.wait()

    @pl.loop(1, devices)
    def _(step):
        sender = lax.rem(me - step + devices, devices)
        pltpu.make_async_remote_copy(
            src_ref=outgoing.at[sender],
            dst_ref=arrived.at[sender],
            send_sem=send_sems.at[step],
            recv_sem=recv_sems.at[step],
            device_id=(sender // grp_size, lax.rem(sender, grp_size)),
            device_id_type=MESH,
        ).wait_recv()

    @pl.loop(1, devices)
    def _(step):
        copy_to(step).wait_send()


def exchange(outgoing, devices, grp_size):
    block = outgoing.shape[1:]
    return pl.pallas_call(
        functools.partial(exchange_kernel, devices, grp_size),
        out_shape=jax.ShapeDtypeStruct(outgoing.shape, outgoing.dtype),
        in_specs=[pl.BlockSpec(memory_space=pl.ANY)],
        out_specs=pl.BlockSpec(memory_space=pl.ANY),
        scratch_shapes=[
            pltpu.VMEM(block, outgoing.dtype),
            pltpu.SemaphoreType.DMA((devices,)),
            pltpu.SemaphoreType.DMA((devices,)),
            pltpu.SemaphoreType.DMA((2,)),
        ],
        compiler_params=pltpu.CompilerParams(has_side_effects=True),
    )(outgoing)


def finish_kernel(count, order, *refs):
    arrived, (rollout, sums) = refs[:count], refs[count:]
    rows = arrived[0].shape[-1]
    blocks = rows // BLOCK
    row_block = lax.broadcasted_iota(jnp.int32, (rows, blocks * count), 0) // BLOCK
    column = lax.broadcasted_iota(jnp.int32, (rows, blocks * count), 1)
    total = None
    for part in range(count):
        values = arrived[part][0, 0]
        rollout[0, :, part * rows : (part + 1) * rows] = values
        chooser = jnp.where(column == row_block + part * blocks, 1.0, 0.0).astype(jnp.bfloat16)
        term = jnp.dot(values, chooser, preferred_element_type=jnp.float32)
        total = term if total is None else total + term
    sums[0] = total


def finish(arrived, row_order):
    devices, layers, col_width, rows = arrived.shape
    blocks = rows // BLOCK
    count = max(1, LANES // blocks)
    if rows % LANES or blocks * count != LANES or devices % count or col_width % 16:
        rollout = jnp.take(arrived, row_order, axis=0).transpose(1, 2, 0, 3)
        rollout = rollout.reshape(layers, col_width, devices * rows)
        sums = rollout.astype(jnp.float32).reshape(layers, col_width, devices * blocks, BLOCK).sum(axis=-1)
        return rollout, sums

    def pick(part):
        return lambda layer, group, order: (order[group * count + part], layer, 0, 0)

    return pl.pallas_call(
        functools.partial(finish_kernel, count),
        grid_spec=pltpu.PrefetchScalarGridSpec(
            num_scalar_prefetch=1,
            grid=(layers, devices // count),
            in_specs=[pl.BlockSpec((1, 1, col_width, rows), pick(part)) for part in range(count)],
            out_specs=[
                pl.BlockSpec((1, col_width, count * rows), lambda layer, group, order: (layer, 0, group)),
                pl.BlockSpec((1, col_width, LANES), lambda layer, group, order: (layer, 0, group)),
            ],
        ),
        out_shape=[
            jax.ShapeDtypeStruct((layers, col_width, devices * rows), jnp.bfloat16),
            jax.ShapeDtypeStruct((layers, col_width, devices * blocks), jnp.float32),
        ],
    )(row_order, *([arrived] * count))


def shards(codes, exponents, column_map, row_order):
    grp_size = lax.axis_size("grp")
    devices = lax.axis_size("chain") * grp_size
    outgoing = prepare(codes, exponents, column_map, devices)
    arrived = exchange(outgoing, devices, grp_size)
    rollout, sums = finish(arrived, row_order)
    return (rollout, sums)


def solution(mesh):
    return jax.shard_map(
        shards,
        mesh=mesh,
        in_specs=(P(None, ("chain", "grp"), None), P(None, ("chain", "grp"), None), P(), P()),
        out_specs=(P(None, ("chain", "grp"), None), P(None, ("chain", "grp"), None)),
        check_vma=False,
    )
```

time: 542 us -> 394 us (0.73)
  Pallas kernels: 0 us -> 391 us
  waiting for transfers between devices: 282 us -> 0 us
  local copies, waits for them, and re-layouts: 175 us -> 0 us
  other arithmetic: 57.2 us -> 1.28 us
  blocking collectives: 14.9 us -> 0 us
  starting transfers between devices: 6.71 us -> 0 us
    pallas_call x0 -> x3, Pallas kernels: none -> 391 us  [the longest x1 348 us: exchange(): pl.pallas_call(functools.partial(exchange_kernel, devices, grp_size), out...]
    all_to_all x1 -> x0, waiting for transfers between devices: 282 us -> none  [shards(): lax.all_to_all(shaped, 'chain', split_axis=2, concat_axis=2, tiled=True)]
    gather x4 -> x0, local copies, waits for them, and re-layouts: 109 us -> none  [the longest x1 67.6 us: arrange(): picked = jnp.take(array, order, axis=2)]
    select_n x4 -> x0, other arithmetic: 34.3 us -> none  [the longest x2 23.6 us: arrange(): picked = jnp.take(array, order, axis=2)]
    convert_element_type x1 -> x0, local copies, waits for them, and re-layouts: 31 us -> none  [shards(): (codes.astype(jnp.float32) * jnp.repeat(scaling, 32, axis=1)).astype(jnp....]
    all_to_all x1 -> x0, blocking collectives: 14.9 us -> none  [shards(): lax.all_to_all(lax.all_to_all(shaped, 'chain', split_axis=2, concat_axis=...]
    all_to_all x1 -> x0, local copies, waits for them, and re-layouts: 13.3 us -> none  [shards(): lax.all_to_all(shaped, 'chain', split_axis=2, concat_axis=2, tiled=True)]
    convert_element_type x1 -> x0, other arithmetic: 11.6 us -> none  [shards(): (codes.astype(jnp.float32) * jnp.repeat(scaling, 32, axis=1)).astype(jnp....]
  transfers between devices with their start and end apart: 1 -> 0, of which waited for: 1 -> 0; matrix products, arithmetic and copies ran while one was open for 0% -> 0% of each run, Pallas kernels for 0% -> 0%
where the time goes in v1:
time: 394 us; the launch traced here: 393 us
  Pallas kernels  391 us (99%)
    pallas_call x1, Pallas kernels, exchange(): pl.pallas_call(functools.partial(exchange_kernel, devices, grp_size), out...  348 us
    pallas_call x1, Pallas kernels, prepare(): pl.pallas_call(prepare_kernel, grid_spec=pltpu.PrefetchScalarGridSpec(num...  28.7 us
    pallas_call x1, Pallas kernels, finish(): pl.pallas_call(functools.partial(finish_kernel, count), grid_spec=pltpu.P...  14 us

profile of v1, /device:TPU:15, one launch (start us, length us, event | category | flops | bytes accessed | tf_op | source)
XLA Modules:
  0.0 393.0 jit_solution(11584918371631084941)
XLA Ops:
  0.6 1.3 select_reduce_fusion.where
  1.9 28.7 %shard_map.59.outgoing = bf16[32,2,192,512]{3,2,1,0:T(8,128)(2,1)} custom-call(s32[32]{0:T(128)} %select_reduce_fusion.where, bf16[2,512,6144]{2,1,0:T(8,128)(2,1)} %codes.1, s32[2,16,6144]{2,1,0:T(8,128)} %exponents.1), custom_call_target="tpu_custom_call" | custom-call | tf_op jit(solution)/shard_map/pallas_call | solution.py:47
  30.6 348.4 %shard_map.60.refs_0_.refs_1_.refs_2_.refs_3_.refs_4_.refs_5_.refs_6_.refs_7_ = bf16[32,2,192,512]{3,2,1,0:T(8,128)(2,1)} custom-call(bf16[32,2,192,512]{3,2,1,0:T(8,128)(2,1)} %shard_map.59.outgoing), custom_call_target="tpu_custom_call" | custom-call | tf_op jit(solution)/shard_map/pallas_call | solution.py:107
  379.0 14.0 %shard_map.61 = (bf16[2,192,16384]{2,1,0:T(8,128)(2,1)}, f32[2,192,512]{2,1,0:T(8,128)}) custom-call(s32[32]{0:T(128)} %order.1, bf16[32,2,192,512]{3,2,1,0:T(8,128)(2,1)} %shard_map.60.refs_0_.refs_1_.refs_2_.refs_3_.refs_4_.refs_5_.refs_6_.refs_7_, bf16[32,2,192,512]{3,2,1,0:T(8,128)(2,1)} %shard_map.60.refs_0_.refs_1_.refs_2_.refs_3_.refs_4_.refs_5_.refs_6_.refs_7_, ...), custom_call_target="tpu_custom_call" | custom-call | tf_op jit(solution)/shard_map/pallas_call | solution.py:151

commit v2 on v1

v2 whole, which is shorter than its diff:
```python
import functools

import jax
import jax.numpy as jnp
from jax import lax
from jax.experimental import pallas as pl
from jax.experimental.pallas import tpu as pltpu
from jax.sharding import PartitionSpec as P

MESH = pl.DeviceIdType.MESH
BLOCK = 32
LANES = 128


def partner(me, step, devices):
    if devices & (devices - 1):
        return lax.rem(me + step, devices)
    peer, bit = 0, 1
    while bit < devices:
        peer = peer + lax.rem(me // bit + step // bit, 2) * bit
        bit *= 2
    return peer


def origin(me, step, devices):
    if devices & (devices - 1):
        return lax.rem(me - step + devices, devices)
    return partner(me, step, devices)


def turn_of(index, devices):
    if devices % 2:
        return index + 1
    odd = lax.rem(index, 2)
    return (index + odd) // 2 + (1 - odd) * (devices // 2)


class Traffic:
    def __init__(self, devices, grp_size, source, arrived, send_sems, recv_sems):
        self.devices, self.grp_size = devices, grp_size
        self.source, self.arrived = source, arrived
        self.send_sems, self.recv_sems = send_sems, recv_sems
        self.me = lax.axis_index("chain") * grp_size + lax.axis_index("grp")

    def copy(self, step, other, slot):
        return pltpu.make_async_remote_copy(
            src_ref=self.source(step, other),
            dst_ref=self.arrived.at[slot],
            send_sem=self.send_sems.at[step],
            recv_sem=self.recv_sems.at[step],
            device_id=(other // self.grp_size, lax.rem(other, self.grp_size)),
            device_id_type=MESH,
        )

    def send(self, step):
        return self.copy(step, partner(self.me, step, self.devices), self.me)

    def finish(self):
        @pl.loop(1, self.devices)
        def _(step):
            sender = origin(self.me, step, self.devices)
            self.copy(step, sender, sender).wait_recv()

        @pl.loop(1, self.devices)
        def _(step):
            self.send(step).wait_send()


def fused_kernel(
    devices, grp_size, column_map, codes, exponents, arrived,
    codes_in, exponents_in, turned, sending, load_sems, send_sems, recv_sems, own_sem,
):
    pairs, layers, rows, pair = codes_in.shape
    col_width = pair // 2

    def loads(index):
        columns = pl.ds(pl.multiple_of(index * pair, LANES), pair)
        return (
            pltpu.make_async_copy(codes.at[:, :, columns], codes_in.at[index], load_sems.at[0, index]),
            pltpu.make_async_copy(exponents.at[:, :, columns], exponents_in.at[index], load_sems.at[1, index]),
        )

    @pl.loop(0, pairs)
    def _(index):
        for load in loads(index):
            load.start()

    @pl.loop(0, pairs)
    def _(index):
        for load in loads(index):
            load.wait()

    traffic = Traffic(
        devices, grp_size, lambda step, other: sending.at[step], arrived, send_sems, recv_sems
    )

    def fill(step):
        column = column_map[partner(traffic.me, step, devices)]
        which = column // 2
        for layer in range(layers):
            scaling = jnp.exp2(exponents_in[which, layer].astype(jnp.float32)).astype(jnp.bfloat16)
            for first in range(0, rows, LANES):
                pieces = []
                for row in range(first, first + LANES, BLOCK):
                    block = row // BLOCK
                    values = codes_in[which, layer, row : row + BLOCK, :]
                    pieces.append(values * scaling[block : block + 1, :])
                both = jnp.concatenate(pieces, axis=0).T
                turned[0, layer, :, first : first + LANES] = both[:col_width]
                turned[1, layer, :, first : first + LANES] = both[col_width:]
        sending[step] = turned[lax.rem(column, 2)]

    fill(turn_of(0, devices))

    @pl.loop(1, devices - 1)
    def _(index):
        fill(turn_of(index, devices))
        traffic.send(turn_of(index - 1, devices)).start()

    fill(0)
    traffic.send(turn_of(devices - 2, devices)).start()
    own = pltpu.make_async_copy(sending.at[0], arrived.at[traffic.me], own_sem)
    own.start()
    own.wait()
    traffic.finish()


def exchange_kernel(devices, grp_size, outgoing, arrived, own, send_sems, recv_sems, own_sems):
    traffic = Traffic(
        devices, grp_size, lambda step, other: outgoing.at[other], arrived, send_sems, recv_sems
    )

    @pl.loop(0, devices - 1)
    def _(index):
        traffic.send(turn_of(index, devices)).start()

    take = pltpu.make_async_copy(outgoing.at[traffic.me], own, own_sems.at[0])
    take.start()
    take.wait()
    put = pltpu.make_async_copy(own, arrived.at[traffic.me], own_sems.at[1])
    put.start()
    put.wait()
    traffic.finish()


def exchange(codes, exponents, column_map, devices, grp_size):
    layers, rows, width = codes.shape
    col_width = width // devices
    block = (layers, col_width, rows)
    shape = jax.ShapeDtypeStruct((devices, *block), jnp.bfloat16)
    anywhere = pl.BlockSpec(memory_space=pl.ANY)
    peers = pltpu.SemaphoreType.DMA((devices,))
    if col_width % 64 or rows % LANES or devices % 2:
        scaling = jnp.exp2(exponents.astype(jnp.float32))
        values = (codes.astype(jnp.float32) * jnp.repeat(scaling, BLOCK, axis=1)).astype(jnp.bfloat16)
        values = values.reshape(layers, rows, devices, col_width)
        outgoing = jnp.take(values.transpose(2, 0, 3, 1), column_map, axis=0)
        return pl.pallas_call(
            functools.partial(exchange_kernel, devices, grp_size),
            out_shape=shape,
            in_specs=[anywhere],
            out_specs=anywhere,
            scratch_shapes=[pltpu.VMEM(block, jnp.bfloat16), peers, peers, pltpu.SemaphoreType.DMA((2,))],
            compiler_params=pltpu.CompilerParams(has_side_effects=True),
        )(outgoing)
    pairs = devices // 2
    return pl.pallas_call(
        functools.partial(fused_kernel, devices, grp_size),
        out_shape=shape,
        in_specs=[pl.BlockSpec(memory_space=pltpu.SMEM), anywhere, anywhere],
        out_specs=anywhere,
        scratch_shapes=[
            pltpu.VMEM((pairs, layers, rows, 2 * col_width), codes.dtype),
            pltpu.VMEM((pairs, layers, rows // BLOCK, 2 * col_width), exponents.dtype),
            pltpu.VMEM((2, *block), jnp.bfloat16),
            pltpu.VMEM((devices, *block), jnp.bfloat16),
            pltpu.SemaphoreType.DMA((2, pairs)),
            peers,
            peers,
            pltpu.SemaphoreType.DMA,
        ],
        compiler_params=pltpu.CompilerParams(has_side_effects=True),
    )(column_map, codes, exponents)


def finish_kernel(count, order, *refs):
    arrived, (rollout, sums) = refs[:count], refs[count:]
    rows = arrived[0].shape[-1]
    blocks = rows // BLOCK
    row_block = lax.broadcasted_iota(jnp.int32, (rows, blocks * count), 0) // BLOCK
    column = lax.broadcasted_iota(jnp.int32, (rows, blocks * count), 1)
    total = None
    for part in range(count):
        values = arrived[part][0, 0]
        rollout[0, :, part * rows : (part + 1) * rows] = values
        chooser = jnp.where(column == row_block + part * blocks, 1.0, 0.0).astype(jnp.bfloat16)
        term = jnp.dot(values, chooser, preferred_element_type=jnp.float32)
        total = term if total is None else total + term
    sums[0] = total


def finish(arrived, row_order):
    devices, layers, col_width, rows = arrived.shape
    blocks = rows // BLOCK
    count = max(1, LANES // blocks)
    if rows % LANES or blocks * count != LANES or devices % count or col_width % 16:
        rollout = jnp.take(arrived, row_order, axis=0).transpose(1, 2, 0, 3)
        rollout = rollout.reshape(layers, col_width, devices * rows)
        sums = rollout.astype(jnp.float32).reshape(layers, col_width, devices * blocks, BLOCK).sum(axis=-1)
        return rollout, sums

    def pick(part):
        return lambda layer, group, order: (order[group * count + part], layer, 0, 0)

    return pl.pallas_call(
        functools.partial(finish_kernel, count),
        grid_spec=pltpu.PrefetchScalarGridSpec(
            num_scalar_prefetch=1,
            grid=(layers, devices // count),
            in_specs=[pl.BlockSpec((1, 1, col_width, rows), pick(part)) for part in range(count)],
            out_specs=[
                pl.BlockSpec((1, col_width, count * rows), lambda layer, group, order: (layer, 0, group)),
                pl.BlockSpec((1, col_width, LANES), lambda layer, group, order: (layer, 0, group)),
            ],
        ),
        out_shape=[
            jax.ShapeDtypeStruct((layers, col_width, devices * rows), jnp.bfloat16),
            jax.ShapeDtypeStruct((layers, col_width, devices * blocks), jnp.float32),
        ],
    )(row_order, *([arrived] * count))


def shards(codes, exponents, column_map, row_order):
    grp_size = lax.axis_size("grp")
    devices = lax.axis_size("chain") * grp_size
    arrived = exchange(codes, exponents, column_map, devices, grp_size)
    rollout, sums = finish(arrived, row_order)
    return (rollout, sums)


def solution(mesh):
    return jax.shard_map(
        shards,
        mesh=mesh,
        in_specs=(P(None, ("chain", "grp"), None), P(None, ("chain", "grp"), None), P(), P()),
        out_specs=(P(None, ("chain", "grp"), None), P(None, ("chain", "grp"), None)),
        check_vma=False,
    )
```

time: 394 us -> 306 us (0.78)
  Pallas kernels: 391 us -> 303 us
    pallas_call x2 -> x1, Pallas kernels: 377 us -> 289 us  [exchange(): pl.pallas_call(functools.partial(fused_kernel, devices, grp_size), out_sh...]
where the time goes in v2:
time: 306 us; the launch traced here: 304 us
  Pallas kernels  303 us (99%)
    pallas_call x1, Pallas kernels, exchange(): pl.pallas_call(functools.partial(fused_kernel, devices, grp_size), out_sh...  289 us
    pallas_call x1, Pallas kernels, finish(): pl.pallas_call(functools.partial(finish_kernel, count), grid_spec=pltpu.P...  14 us

profile of v2, /device:TPU:15, one launch (start us, length us, event | category | flops | bytes accessed | tf_op | source)
XLA Modules:
  0.0 303.9 jit_solution(5531018290373345067)
XLA Ops:
  0.6 289.3 %shard_map.59.refs_0_.refs_1_.refs_2_.refs_3_.refs_4_.refs_5_.refs_6_.refs_7_ = bf16[32,2,192,512]{3,2,1,0:T(8,128)(2,1)} custom-call(s32[32]{0:T(128)} %column_map.1, bf16[2,512,6144]{2,1,0:T(8,128)(2,1)} %codes.1, s32[2,16,6144]{2,1,0:T(8,128)} %exponents.1), custom_call_target="tpu_custom_call" | custom-call | tf_op jit(solution)/shard_map/pallas_call | solution.py:167
  289.9 14.0 %shard_map.60 = (bf16[2,192,16384]{2,1,0:T(8,128)(2,1)}, f32[2,192,512]{2,1,0:T(8,128)}) custom-call(s32[32]{0:T(128)} %order.1, bf16[32,2,192,512]{3,2,1,0:T(8,128)(2,1)} %shard_map.59.refs_0_.refs_1_.refs_2_.refs_3_.refs_4_.refs_5_.refs_6_.refs_7_, bf16[32,2,192,512]{3,2,1,0:T(8,128)(2,1)} %shard_map.59.refs_0_.refs_1_.refs_2_.refs_3_.refs_4_.refs_5_.refs_6_.refs_7_, ...), custom_call_target="tpu_custom_call" | custom-call | tf_op jit(solution)/shard_map/pallas_call | solution.py:215

commit v3 on v2

v3 whole, which is shorter than its diff:
```python
import functools

import jax
import jax.numpy as jnp
from jax import lax
from jax.experimental import pallas as pl
from jax.experimental.pallas import tpu as pltpu
from jax.sharding import PartitionSpec as P

MESH = pl.DeviceIdType.MESH
BLOCK = 32
LANES = 128


def partner(me, step, devices):
    if devices & (devices - 1):
        return lax.rem(me + step, devices)
    peer, bit = 0, 1
    while bit < devices:
        peer = peer + lax.rem(me // bit + step // bit, 2) * bit
        bit *= 2
    return peer


def origin(me, step, devices):
    if devices & (devices - 1):
        return lax.rem(me - step + devices, devices)
    return partner(me, step, devices)


def turn_of(index, devices):
    if devices % 2:
        return index + 1
    odd = lax.rem(index, 2)
    return (index + odd) // 2 + (1 - odd) * (devices // 2)


class Traffic:
    def __init__(self, devices, grp_size, layers, source, arrived, send_sems, recv_sems):
        self.devices, self.grp_size, self.layers = devices, grp_size, layers
        self.source, self.arrived = source, arrived
        self.send_sems, self.recv_sems = send_sems, recv_sems
        self.me = lax.axis_index("chain") * grp_size + lax.axis_index("grp")

    def copy(self, step, layer, other, slot):
        return pltpu.make_async_remote_copy(
            src_ref=self.source(step, layer, other),
            dst_ref=self.arrived.at[slot, layer],
            send_sem=self.send_sems.at[step, layer],
            recv_sem=self.recv_sems.at[step, layer],
            device_id=(other // self.grp_size, lax.rem(other, self.grp_size)),
            device_id_type=MESH,
        )

    def send(self, step, layer):
        return self.copy(step, layer, partner(self.me, step, self.devices), self.me)

    def finish(self):
        @pl.loop(1, self.devices)
        def _(step):
            sender = origin(self.me, step, self.devices)
            for layer in range(self.layers):
                self.copy(step, layer, sender, sender).wait_recv()

        @pl.loop(1, self.devices)
        def _(step):
            for layer in range(self.layers):
                self.send(step, layer).wait_send()


def fused_kernel(devices, grp_size, layers, column_map, codes, exponents, arrived, *scratch):
    codes_in, exponents_in = scratch[:layers], scratch[layers : 2 * layers]
    turned, sending, load_sems, send_sems, recv_sems, own_sem = scratch[2 * layers :]
    pairs, rows, pair = codes_in[0].shape
    col_width = pair // 2

    def loads(layer, index):
        columns = pl.ds(pl.multiple_of(index * pair, LANES), pair)
        return (
            pltpu.make_async_copy(
                codes.at[layer, :, columns], codes_in[layer].at[index], load_sems.at[0, layer, index]
            ),
            pltpu.make_async_copy(
                exponents.at[layer, :, columns], exponents_in[layer].at[index], load_sems.at[1, layer, index]
            ),
        )

    def load(layer):
        @pl.loop(0, pairs)
        def _(index):
            for item in loads(layer, index):
                item.start()

    def loaded(layer):
        @pl.loop(0, pairs)
        def _(index):
            for item in loads(layer, index):
                item.wait()

    traffic = Traffic(
        devices, grp_size, layers, lambda step, layer, other: sending.at[step, layer], arrived, send_sems, recv_sems
    )

    def fill(step, layer):
        column = column_map[partner(traffic.me, step, devices)]
        which = column // 2
        scaling = jnp.exp2(exponents_in[layer][which].astype(jnp.float32)).astype(jnp.bfloat16)
        for first in range(0, rows, LANES):
            pieces = []
            for row in range(first, first + LANES, BLOCK):
                block = row // BLOCK
                pieces.append(codes_in[layer][which, row : row + BLOCK, :] * scaling[block : block + 1, :])
            both = jnp.concatenate(pieces, axis=0).T
            turned[0, :, first : first + LANES] = both[:col_width]
            turned[1, :, first : first + LANES] = both[col_width:]
        sending[step, layer] = turned[lax.rem(column, 2)]

    for layer in range(layers):
        load(layer)
    for layer in range(layers):
        loaded(layer)
        fill(turn_of(0, devices), layer)
        if layer:
            traffic.send(turn_of(0, devices), layer - 1).start()

    @pl.loop(1, devices - 1)
    def _(index):
        for layer in range(layers):
            fill(turn_of(index, devices), layer)
            if layer:
                traffic.send(turn_of(index, devices), layer - 1).start()
            else:
                traffic.send(turn_of(index - 1, devices), layers - 1).start()

    for layer in range(layers):
        fill(0, layer)
    traffic.send(turn_of(devices - 2, devices), layers - 1).start()
    own = pltpu.make_async_copy(sending.at[0], arrived.at[traffic.me], own_sem)
    own.start()
    own.wait()
    traffic.finish()


def exchange_kernel(devices, grp_size, layers, outgoing, arrived, own, send_sems, recv_sems, own_sems):
    traffic = Traffic(
        devices, grp_size, layers, lambda step, layer, other: outgoing.at[other, layer], arrived, send_sems, recv_sems
    )

    @pl.loop(0, devices - 1)
    def _(index):
        for layer in range(layers):
            traffic.send(turn_of(index, devices), layer).start()

    take = pltpu.make_async_copy(outgoing.at[traffic.me], own, own_sems.at[0])
    take.start()
    take.wait()
    put = pltpu.make_async_copy(own, arrived.at[traffic.me], own_sems.at[1])
    put.start()
    put.wait()
    traffic.finish()


def exchange(codes, exponents, column_map, devices, grp_size):
    layers, rows, width = codes.shape
    col_width = width // devices
    block = (layers, col_width, rows)
    shape = jax.ShapeDtypeStruct((devices, *block), jnp.bfloat16)
    anywhere = pl.BlockSpec(memory_space=pl.ANY)
    peers = pltpu.SemaphoreType.DMA((devices, layers))
    if col_width % 64 or rows % LANES or devices % 2:
        scaling = jnp.exp2(exponents.astype(jnp.float32))
        values = (codes.astype(jnp.float32) * jnp.repeat(scaling, BLOCK, axis=1)).astype(jnp.bfloat16)
        values = values.reshape(layers, rows, devices, col_width)
        outgoing = jnp.take(values.transpose(2, 0, 3, 1), column_map, axis=0)
        return pl.pallas_call(
            functools.partial(exchange_kernel, devices, grp_size, layers),
            out_shape=shape,
            in_specs=[anywhere],
            out_specs=anywhere,
            scratch_shapes=[pltpu.VMEM(block, jnp.bfloat16), peers, peers, pltpu.SemaphoreType.DMA((2,))],
            compiler_params=pltpu.CompilerParams(has_side_effects=True),
        )(outgoing)
    pairs = devices // 2
    return pl.pallas_call(
        functools.partial(fused_kernel, devices, grp_size, layers),
        out_shape=shape,
        in_specs=[pl.BlockSpec(memory_space=pltpu.SMEM), anywhere, anywhere],
        out_specs=anywhere,
        scratch_shapes=[
            *[pltpu.VMEM((pairs, rows, 2 * col_width), codes.dtype)] * layers,
            *[pltpu.VMEM((pairs, rows // BLOCK, 2 * col_width), exponents.dtype)] * layers,
            pltpu.VMEM((2, col_width, rows), jnp.bfloat16),
            pltpu.VMEM((devices, *block), jnp.bfloat16),
            pltpu.SemaphoreType.DMA((2, layers, pairs)),
            peers,
            peers,
            pltpu.SemaphoreType.DMA,
        ],
        compiler_params=pltpu.CompilerParams(has_side_effects=True),
    )(column_map, codes, exponents)


def finish_kernel(count, order, *refs):
    arrived, (rollout, sums, chooser) = refs[:count], refs[count:]
    rows = arrived[0].shape[-1]
    blocks = rows // BLOCK

    @pl.when((pl.program_id(0) == 0) & (pl.program_id(1) == 0))
    def _():
        row_block = lax.broadcasted_iota(jnp.int32, (rows, blocks * count), 0) // BLOCK
        column = lax.broadcasted_iota(jnp.int32, (rows, blocks * count), 1)
        for part in range(count):
            chosen = column == row_block + part * blocks
            chooser[part] = jnp.where(chosen, 1.0, 0.0).astype(jnp.bfloat16)

    total = None
    for part in range(count):
        values = arrived[part][0, 0]
        rollout[0, :, part * rows : (part + 1) * rows] = values
        term = jnp.dot(values, chooser[part], preferred_element_type=jnp.float32)
        total = term if total is None else total + term
    sums[0] = total


def finish(arrived, row_order):
    devices, layers, col_width, rows = arrived.shape
    blocks = rows // BLOCK
    count = max(1, LANES // blocks)
    if rows % LANES or blocks * count != LANES or devices % count or col_width % 16:
        rollout = jnp.take(arrived, row_order, axis=0).transpose(1, 2, 0, 3)
        rollout = rollout.reshape(layers, col_width, devices * rows)
        sums = rollout.astype(jnp.float32).reshape(layers, col_width, devices * blocks, BLOCK).sum(axis=-1)
        return rollout, sums

    def pick(part):
        return lambda layer, group, order: (order[group * count + part], layer, 0, 0)

    return pl.pallas_call(
        functools.partial(finish_kernel, count),
        grid_spec=pltpu.PrefetchScalarGridSpec(
            num_scalar_prefetch=1,
            grid=(layers, devices // count),
            in_specs=[pl.BlockSpec((1, 1, col_width, rows), pick(part)) for part in range(count)],
            out_specs=[
                pl.BlockSpec((1, col_width, count * rows), lambda layer, group, order: (layer, 0, group)),
                pl.BlockSpec((1, col_width, LANES), lambda layer, group, order: (layer, 0, group)),
            ],
            scratch_shapes=[pltpu.VMEM((count, rows, LANES), jnp.bfloat16)],
        ),
        out_shape=[
            jax.ShapeDtypeStruct((layers, col_width, devices * rows), jnp.bfloat16),
            jax.ShapeDtypeStruct((layers, col_width, devices * blocks), jnp.float32),
        ],
    )(row_order, *([arrived] * count))


def shards(codes, exponents, column_map, row_order):
    grp_size = lax.axis_size("grp")
    devices = lax.axis_size("chain") * grp_size
    arrived = exchange(codes, exponents, column_map, devices, grp_size)
    rollout, sums = finish(arrived, row_order)
    return (rollout, sums)


def solution(mesh):
    return jax.shard_map(
        shards,
        mesh=mesh,
        in_specs=(P(None, ("chain", "grp"), None), P(None, ("chain", "grp"), None), P(), P()),
        out_specs=(P(None, ("chain", "grp"), None), P(None, ("chain", "grp"), None)),
        check_vma=False,
    )
```

time: 306 us -> 306 us (level)
  no operation moved by 1% of the time
where the time goes in v3:
time: 306 us; the launch traced here: 304 us
  Pallas kernels  304 us (99%)
    pallas_call x1, Pallas kernels, exchange(): pl.pallas_call(functools.partial(fused_kernel, devices, grp_size, layers)...  290 us
    pallas_call x1, Pallas kernels, finish(): pl.pallas_call(functools.partial(finish_kernel, count), grid_spec=pltpu.P...  13.8 us

profile of v3, /device:TPU:15, one launch (start us, length us, event | category | flops | bytes accessed | tf_op | source)
XLA Modules:
  0.0 304.3 jit_solution(2818772235094633174)
XLA Ops:
  0.6 289.8 %shard_map.59.refs_0_.refs_1_.refs_2_.refs_3_.refs_4_.refs_5_.refs_6_.refs_7_ = bf16[32,2,192,512]{3,2,1,0:T(8,128)(2,1)} custom-call(s32[32]{0:T(128)} %column_map.1, bf16[2,512,6144]{2,1,0:T(8,128)(2,1)} %codes.1, s32[2,16,6144]{2,1,0:T(8,128)} %exponents.1), custom_call_target="tpu_custom_call" | custom-call | tf_op jit(solution)/shard_map/pallas_call | solution.py:184
  290.5 13.8 %shard_map.60 = (bf16[2,192,16384]{2,1,0:T(8,128)(2,1)}, f32[2,192,512]{2,1,0:T(8,128)}) custom-call(s32[32]{0:T(128)} %order.1, bf16[32,2,192,512]{3,2,1,0:T(8,128)(2,1)} %shard_map.59.refs_0_.refs_1_.refs_2_.refs_3_.refs_4_.refs_5_.refs_6_.refs_7_, bf16[32,2,192,512]{3,2,1,0:T(8,128)(2,1)} %shard_map.59.refs_0_.refs_1_.refs_2_.refs_3_.refs_4_.refs_5_.refs_6_.refs_7_, ...), custom_call_target="tpu_custom_call" | custom-call | tf_op jit(solution)/shard_map/pallas_call | solution.py:238
